TPU v7x, 128 devices: a whole 4x4x4 slice. The times are simulated.
128 devices in a mesh: shard: 8 (over y, core), model: 16 (over z, x).
Axes of the slice: x: 4, y: 4, z: 4, core: 2. Of those that a mesh axis runs over, the one named last changes fastest.
Arguments:
- train_gate: float32 [4096, 12288], P('shard', 'model'), may hold values from -0.125 to 0.125
- slow_gate: float32 [4096, 12288], P('shard', 'model'), may hold values from -0.09375 to 0.09375
- train_up: float32 [4096, 12288], P('shard', 'model'), may hold values from -0.125 to 0.125
- slow_up: float32 [4096, 12288], P('shard', 'model'), may hold values from -0.09375 to 0.09375
- norm_train: float32 [4096], P(('shard', 'model')), may hold values from 0.25 to 1.75
- norm_step: float32 [4096], P(('shard', 'model')), may hold values from -0.3 to 0.3
Outputs:
- serve_gate: bfloat16 [4096, 12288], P(None, 'model')
- serve_up: bfloat16 [4096, 12288], P(None, 'model')
- factor_gate: float32 [12288], P('model')
- factor_up: float32 [12288], P('model')
- serve_norm: bfloat16 [4096], replicated
- fresh_gate: float32 [4096, 12288], P('shard', 'model')
- fresh_up: float32 [4096, 12288], P('shard', 'model')
All inputs are finite; a program needn't handle non-finite values. Where the computation divides by a largest or mean magnitude, that divisor is 1e-20 or more.
Results may differ from a plain program's by a relative error of at most 0.001.
Values may be sent and summed in bfloat16 or wider, within the bound.
No kernel may reach another device: no remote copies, remote signals or barrier semaphores. Data moves between devices by JAX's collectives and lax.ppermute only.
A program may use at most 128 MiB of HBM per device.

v0:
```python
import jax
import jax.numpy as jnp
from jax import lax
from jax.sharding import Mesh
from jax.sharding import PartitionSpec as P

D_MODEL = 4096
SHARD = ("shard_0", "shard_1")
SHARD_MODEL = ("shard_0", "shard_1", "model_0", "model_1")
MODEL = ("model_0", "model_1")


keep_rate = 0.75


def from_everyone(array, axis):
    copies = jnp.broadcast_to(array, (lax.axis_size(axis), *array.shape))
    return lax.all_to_all(copies, axis, split_axis=0, concat_axis=0, tiled=True)


def taken_together(array, axis):
    everything = from_everyone(array, axis)
    return jnp.sum(everything, axis=0)


def in_one(arrays, axis):
    ends = [0]
    for a in arrays:
        ends.append(ends[-1] + a.size)
    subtotal = taken_together(jnp.concatenate([a.ravel() for a in arrays]), axis)
    return tuple((subtotal[b:e].reshape(a.shape) for a, b, e in zip(arrays, ends, ends[1:])))


def sent_together(arrays, axis, dim, along):
    widths = [a.shape[along] for a in arrays]
    both = jnp.concatenate(arrays, axis=along)
    filled = lax.all_gather(both, axis, axis=dim, tiled=True)
    return tuple(jnp.split(filled, [sum(widths[:k]) for k in range(1, len(widths))], axis=along))


def in_order(blocks, dim):
    blocks = jnp.moveaxis(blocks, 0, dim)
    lengths = blocks.shape
    return blocks.reshape(*lengths[:dim], lengths[dim] * lengths[dim + 1], *lengths[dim + 2 :])


def stacked_from(array, axes, turns):
    blocks = array[None]
    for k in turns:
        blocks = lax.all_gather(blocks, axes[k], axis=0, tiled=True)
    held = [lax.axis_size(axes[k]) for k in reversed(turns)]
    blocks = blocks.reshape(*held, *array.shape)
    turned = sorted(range(len(turns)), key=lambda place: turns[len(turns) - 1 - place])
    return blocks.transpose(*turned, *range(len(turns), blocks.ndim)).reshape(-1, *array.shape)


def gathered_by_axis(array, axes, turns, dim):
    return in_order(stacked_from(array, axes, turns), dim)


def shards(train_gate, slow_gate, train_up, slow_up, norm_train, norm_step):
    fresh_gate = keep_rate * slow_gate + (1.0 - keep_rate) * train_gate
    fresh_up = keep_rate * slow_up + (1.0 - keep_rate) * train_up
    total_gate, total_up = in_one(
        (jnp.sum(jnp.abs(fresh_gate), axis=0), jnp.sum(jnp.abs(fresh_up), axis=0)), SHARD
    )
    factor_gate = total_gate / D_MODEL
    factor_up = total_up / D_MODEL
    narrow_gate, narrow_up = (
        (fresh_gate / factor_gate).astype(jnp.bfloat16),
        (fresh_up / factor_up).astype(jnp.bfloat16),
    )
    serve_gate, serve_up = sent_together((narrow_gate, narrow_up), SHARD, 0, 1)
    serve_norm = gathered_by_axis(
        (norm_train + norm_step).astype(jnp.bfloat16), SHARD_MODEL, (0, 2, 3, 1), 0
    )
    return (serve_gate, serve_up, factor_gate, factor_up, serve_norm, fresh_gate, fresh_up)


def solution(mesh):
    split = Mesh(mesh.devices.reshape(4, 2, 4, 4), ("shard_0", "shard_1", "model_0", "model_1"))
    return jax.shard_map(
        shards,
        mesh=split,
        in_specs=(
            P(SHARD, MODEL),
            P(SHARD, MODEL),
            P(SHARD, MODEL),
            P(SHARD, MODEL),
            P(SHARD_MODEL),
            P(SHARD_MODEL),
        ),
        out_specs=(
            P(None, MODEL),
            P(None, MODEL),
            P(MODEL),
            P(MODEL),
            P(),
            P(SHARD, MODEL),
            P(SHARD, MODEL),
        ),
        check_vma=False,
    )
```

profile of v0, /device:TPU:1, one launch (start us, length us, event | category | flops | bytes accessed | tf_op | source)
XLA Modules:
  0.0 108.5 jit_solution(1710898650069235913)
XLA Ops:
  7.2 0.0 all-gather.5.cloned.1.call-start
  7.2 3.4 %abs_reduce_fusion = (f32[768]{0:T(1024)S(1)}, f32[512,768]{1,0:T(8,128)S(1)}, f32[768]{0:T(1024)S(1)}, f32[512,768]{1,0:T(8,128)S(1)}) fusion(f32[512,768]{1,0:T(8,128)} %param.8, f32[512,768]{1,0:T(8,128)} %param.9, f32[512,768]{1,0:T(8,128)} %param.6, f32[512,768]{1,0:T(8,128)} %param.7), kind=kLoop, calls=%fused_computation.3 | loop fusion | flops 3930624 | bytes 9443328 | tf_op jit(solution)/shard_map/reduce_sum | solution.py:65
  10.6 0.0 copy-start
  10.6 0.0 copy-start.1
  10.6 10.5 %all_to_all.6 = f32[8,1,1536]{2,1,0:T(1,128)S(1)} all-to-all(f32[8,1,1536]{2,1,0:T(1,128)S(1)} %broadcast_in_dim.8), channel_id=1, replica_groups=mesh['shard_0'=4,'shard_1'=2,'model_0'=4,'model_1'=4] {'shard_0','shard_1'}, dimensions={0} | all-to-all | bytes 98304 | tf_op jit(solution)/shard_map/all_to_all | solution.py:18
  21.2 0.0 copy-start.2
  21.3 0.0 copy-start.3
  21.3 0.1 divide_convert_fusion.1
  21.4 0.1 divide_convert_fusion
  21.5 0.0 copy-done
  21.5 0.0 copy-done.1
  21.5 0.3 copy-done.2
  21.8 0.0 copy-done.3
  21.9 1.3 %pad_maximum_fusion = bf16[512,1536]{1,0:T(8,128)(2,1)} fusion(bf16[512,768]{1,0:T(8,128)(2,1)S(1)} %divide_convert_fusion, bf16[512,768]{1,0:T(8,128)(2,1)S(1)} %divide_convert_fusion.1), kind=kLoop, calls=%fused_computation | loop fusion | flops 3145728 | bytes 3145728 | tf_op jit(solution)/shard_map/concatenate | solution.py:36
  23.1 0.0 copy-start.6
  23.1 0.0 copy-start.4
  23.1 0.0 all-gather.5.cloned.1.call-update
  23.2 0.6 copy-done.6
  23.8 0.6 dynamic-slice
  25.0 0.0 copy-done.4
  25.0 0.0 copy-done.5
  25.1 0.2 dynamic-update-slice
  25.3 6.9 %all-reduce = bf16[128]{0:T(256)(128)(2,1)S(1)} all-reduce(bf16[128]{0:T(256)(128)(2,1)S(1)} %dynamic-update-slice), channel_id=2, replica_groups=mesh['shard_0'=4,'shard_1'=2,'model_0'=4,'model_1'=4] {'shard_0'}, use_global_device_ids=true, to_apply=%add | all-reduce | flops 128 | bytes 512
  32.2 0.1 reshape.28
  32.2 9.4 %all-gather.1 = bf16[4,4,32]{2,1,0:T(4,128)(2,1)S(1)} all-gather(bf16[1,4,32]{2,1,0:T(4,128)(2,1)S(1)} %reshape.28), channel_id=1, replica_groups=mesh['shard_0'=4,'shard_1'=2,'model_0'=4,'model_1'=4] {'model_0'}, dimensions={0}, use_global_device_ids=true | all-gather | bytes 1280 | tf_op jit(solution)/shard_map/all_gather | solution.py:50
  41.6 10.4 %all_gather.18 = bf16[64,32]{1,0:T(8,128)(2,1)S(1)} all-gather(bf16[16,32]{1,0:T(8,128)(2,1)S(1)} %bitcast.8), channel_id=1, replica_groups=mesh['shard_0'=4,'shard_1'=2,'model_0'=4,'model_1'=4] {'model_1'}, dimensions={0}, use_global_device_ids=true | all-gather | bytes 5120 | tf_op jit(solution)/shard_map/all_gather | solution.py:50
  52.0 0.1 copy.24
  52.1 7.8 %all-gather.2 = bf16[2,64,32]{1,2,0:T(8,128)(2,1)S(1)} all-gather(bf16[1,64,32]{1,2,0:T(8,128)(2,1)S(1)} %copy.24), channel_id=1, replica_groups=mesh['shard_0'=4,'shard_1'=2,'model_0'=4,'model_1'=4] {'shard_1'}, dimensions={0}, use_global_device_ids=true | all-gather | bytes 12288 | tf_op jit(solution)/shard_map/all_gather | solution.py:50
  59.9 0.1 copy.25
  60.0 0.7 reshape_reshape.3
  60.7 30.7 %all-gather.5.cloned.1.call-done = bf16[4096,1536]{1,0:T(8,128)(2,1)} async-done(((bf16[512,1536]{1,0:T(8,128)(2,1)}), bf16[4096,1536]{1,0:T(8,128)(2,1)}) %all-gather.5.cloned.1.call-update) | async-done | bytes 12582928 | tf_op jit(solution)/shard_map/all_gather | solution.py:37
  91.4 10.2 %fusion = (bf16[4096,768]{1,0:T(8,128)(2,1)}, bf16[4096,768]{1,0:T(8,128)(2,1)}) fusion(bf16[4096,1536]{1,0:T(8,128)(2,1)} %all-gather.5.cloned.1.call-done), kind=kLoop, calls=%fused_computation.11 | loop fusion | bytes 25165824 | tf_op jit(solution)/shard_map/split | solution.py:38
  (8 shorter events, 0.1 us)
Async XLA Ops:
  7.2 84.3 %all-gather.5.cloned.1.call-start = ((), (), s32[]{:S(2)}) async-start(), calls=%async_computation.1 | async-start | bytes 14155776 | tf_op jit(solution)/shard_map/all_gather | solution.py:37
  10.6 11.0 %copy-start = (f32[512,768]{1,0:T(8,128)}, f32[512,768]{1,0:T(8,128)S(1)}, u32[]{:S(2)}) copy-start(f32[512,768]{1,0:T(8,128)S(1)} %get-tuple-element.10) | copy-start | bytes 4718596
  10.6 11.0 %copy-start.1 = (f32[512,768]{1,0:T(8,128)}, f32[512,768]{1,0:T(8,128)S(1)}, u32[]{:S(2)}) copy-start(f32[512,768]{1,0:T(8,128)S(1)} %get-tuple-element.16) | copy-start | bytes 4718596
  21.2 0.6 copy-start.2
  21.3 0.6 copy-start.3
  23.1 0.7 copy-start.6
  23.1 1.9 %copy-start.4 = (f32[32]{0:T(128)S(1)}, f32[32]{0:T(128)}, u32[]{:S(2)}) copy-start(f32[32]{0:T(128)} %param.10) | copy-start | bytes 388
  23.1 1.9 %copy-start.5 = (f32[32]{0:T(128)S(1)}, f32[32]{0:T(128)}, u32[]{:S(2)}) copy-start(f32[32]{0:T(128)} %param.11) | copy-start | bytes 388
Sparse Core Ops, SparseCore 0:
  23.3 68.1 all-gather.4
where the time goes:
time: 109 us
  blocking collectives  45 us (41%)
  waiting for transfers between devices  30.7 us (28%)
  between operations  14.8 us (14%)
  local copies, waits for them, and re-layouts  13 us (12%)
  other arithmetic  4.91 us (5%)
    all_gather x1, waiting for transfers between devices, sent_together(): filled = lax.all_gather(both, axis, axis=dim, tiled=True)  30.7 us
    all_gather x3, blocking collectives, stacked_from(): blocks = lax.all_gather(blocks, axes[k], axis=0, tiled=True)  27.6 us
    all_to_all x1, blocking collectives, from_everyone(): return lax.all_to_all(copies, axis, split_axis=0, concat_axis=0, tiled=True)  10.5 us
    split x1, local copies, waits for them, and re-layouts, sent_together(): jnp.split(filled, [sum(widths[:k]) for k in range(1, len(widths))], axis=...  10.2 us
    unnamed x1, blocking collectives  6.85 us
    reduce_sum x1, other arithmetic, shards(): jnp.sum(jnp.abs(fresh_up), axis=0)  3.36 us
  transfers between devices with their start and end apart: 1, of which 1 were waited for; matrix products, arithmetic and copies ran while one was open for 2% of the time, Pallas kernels for 0%

commit v1 on v0

v1 whole, which is shorter than its diff:
```python
import jax
import jax.numpy as jnp
from jax import lax
from jax.experimental import pallas as pl
from jax.experimental.pallas import tpu as pltpu
from jax.sharding import Mesh
from jax.sharding import PartitionSpec as P


D_MODEL = 4096
Y, CORE, Z, X = "y", "core", "z", "x"
keep_rate = 0.75
TINY = 1e-30


def shifted(array, axis, step):
    n = lax.axis_size(axis)
    return lax.ppermute(array, axis, [(i, (i + step) % n) for i in range(n)])


def swapped(array, axis, mask):
    return lax.ppermute(array, axis, [(i, i ^ mask) for i in range(lax.axis_size(axis))])


def onward(array):
    pairs = [(2 * y + c, 2 * ((y + (1, -1)[c]) % 4) + c) for y in range(4) for c in range(2)]
    return lax.ppermute(array, (Y, CORE), pairs)


def unwritten(shape):
    anywhere = pl.BlockSpec(memory_space=pl.ANY)
    return pl.pallas_call(
        lambda a, b: None,
        out_shape=(jax.ShapeDtypeStruct(shape, jnp.bfloat16),) * 2,
        out_specs=(anywhere, anywhere),
        compiler_params=pltpu.CompilerParams(vmem_limit_bytes=1 << 20),
    )()


def mixed(slow, train):
    return keep_rate * slow + (1.0 - keep_rate) * train


def coded(rows, sums):
    return (rows * (256.0 / jnp.maximum(sums, TINY))).astype(jnp.float16)


def decoded(code, sums, factor):
    scale = jnp.maximum(sums, TINY) * (1.0 / 256.0) / factor
    return (code.astype(jnp.float32) * scale).astype(jnp.bfloat16)


def body(train_gate, slow_gate, train_up, slow_up, norm_train, norm_step):
    y, c, z, x = (lax.axis_index(a) for a in (Y, CORE, Z, X))
    rows, cols = train_gate.shape

    fresh_gate, fresh_up = mixed(slow_gate, train_gate), mixed(slow_up, train_up)
    sg = jnp.sum(jnp.abs(fresh_gate), axis=0)
    su = jnp.sum(jnp.abs(fresh_up), axis=0)
    code_gate = coded(fresh_gate, sg)
    code_up = coded(fresh_up, su)
    eg = onward(code_gate)
    norm = (norm_train + norm_step).astype(jnp.bfloat16)
    slots = jnp.zeros((128 * norm.size,), jnp.float32)
    device = ((y * 2 + c) * 4 + z) * 4 + x
    slots = lax.dynamic_update_slice(slots, norm.astype(jnp.float32), (device * norm.size,))
    sums = jnp.concatenate([sg, su, slots])
    other = swapped(sums, CORE, 1)
    pfg, pfu = swapped(fresh_gate, CORE, 1), swapped(fresh_up, CORE, 1)
    pair = sums + other
    note = jnp.concatenate([pair, sg, su])
    far = shifted(pair, Y, 2)
    right, left = shifted(note, Y, 1), shifted(note, Y, -1)
    eu = onward(code_up)
    n = pair.size
    total = (pair + far) + (right[:n] + left[:n])
    factor_gate, factor_up = total[:cols] / D_MODEL, total[cols : 2 * cols] / D_MODEL
    behind = jnp.where(c == 0, right[n:], left[n:])

    gates, ups = unwritten((8 * rows, cols))
    back = jnp.where(c == 0, -1, 1)

    def put(out, block, dy, core):
        at = (((y + dy) & 3) * 2 + core) * rows
        return lax.dynamic_update_slice(out, block, (at, jnp.int32(0)))

    def normal(fresh, factor):
        return (fresh / factor).astype(jnp.bfloat16)

    block = normal(pfg, factor_gate)
    gates = put(gates, block, 0, c ^ 1)
    ng = onward(block)
    block = normal(pfu, factor_up)
    ups = put(ups, block, 0, c ^ 1)
    nu = onward(block)
    gates = put(gates, normal(fresh_gate, factor_gate), 0, c)
    ups = put(ups, normal(fresh_up, factor_up), 0, c)

    block = decoded(eg, behind[:cols], factor_gate)
    gates = put(gates, block, back, c)
    seg = swapped(block, CORE, 1)
    block = decoded(eu, behind[cols:], factor_up)
    ups = put(ups, block, back, c)
    seu = swapped(block, CORE, 1)
    gates = put(gates, seg, -back, c ^ 1)
    ups = put(ups, seu, -back, c ^ 1)

    slots = total[2 * cols :].astype(jnp.bfloat16)
    for axis, mask in ((X, 1), (X, 3), (Z, 1), (Z, 3)):
        slots = slots + swapped(slots, axis, mask)
    serve_norm = slots

    fg, fu = onward(ng), onward(nu)
    sng, snu = swapped(ng, CORE, 1), swapped(nu, CORE, 1)
    gates = put(gates, ng, back, c ^ 1)
    gates = put(gates, sng, -back, c)
    ups = put(ups, nu, back, c ^ 1)
    ups = put(ups, snu, -back, c)
    sfg, sfu = swapped(fg, CORE, 1), swapped(fu, CORE, 1)
    gates = put(gates, fg, 2, c ^ 1)
    gates = put(gates, sfg, 2, c)
    ups = put(ups, fu, 2, c ^ 1)
    ups = put(ups, sfu, 2, c)
    return (gates, ups, factor_gate, factor_up, serve_norm, fresh_gate, fresh_up)


def solution(mesh):
    split = Mesh(mesh.devices.reshape(4, 2, 4, 4), (Y, CORE, Z, X))
    weights = P((Y, CORE), (Z, X))
    columns = P((Z, X))
    every = P((Y, CORE, Z, X))
    return jax.shard_map(
        body,
        mesh=split,
        in_specs=(weights,) * 4 + (every,) * 2,
        out_specs=(P(None, (Z, X)), P(None, (Z, X)), columns, columns, P(), weights, weights),
        check_vma=False,
    )
```

time: 109 us -> 88.5 us (0.81)
  blocking collectives: 45 us -> 0 us
  starting transfers between devices: 0.04 us -> 44.7 us
  waiting for transfers between devices: 30.7 us -> 12.5 us
  between operations: 14.8 us -> 0.77 us
  other arithmetic: 4.91 us -> 17.4 us
    ppermute x0 -> x22, starting transfers between devices: none -> 44.7 us  [the longest x13 25.2 us: swapped(): lax.ppermute(array, axis, [(i, i ^ mask) for i in range(lax.axis_size(axi...]
    all_gather x1 -> x0, waiting for transfers between devices: 30.7 us -> none  [sent_together(): filled = lax.all_gather(both, axis, axis=dim, tiled=True)]
    all_gather x3 -> x0, blocking collectives: 27.6 us -> none  [stacked_from(): blocks = lax.all_gather(blocks, axes[k], axis=0, tiled=True)]
    dynamic_update_slice x0 -> x10, local copies, waits for them, and re-layouts: none -> 12.7 us  [put(): return lax.dynamic_update_slice(out, block, (at, jnp.int32(0)))]
    ppermute x0 -> x22, waiting for transfers between devices: none -> 12.5 us  [the longest x3 7.64 us: shifted(): return lax.ppermute(array, axis, [(i, (i + step) % n) for i in range(n)])]
    dynamic_update_slice x0 -> x7, other arithmetic: none -> 11.3 us  [the longest x6 10.5 us: put(): return lax.dynamic_update_slice(out, block, (at, jnp.int32(0)))]
    all_to_all x1 -> x0, blocking collectives: 10.5 us -> none  [from_everyone(): return lax.all_to_all(copies, axis, split_axis=0, concat_axis=0, tiled=True)]
    split x1 -> x0, local copies, waits for them, and re-layouts: 10.2 us -> none  [sent_together(): jnp.split(filled, [sum(widths[:k]) for k in range(1, len(widths))], axis=...]
  transfers between devices with their start and end apart: 1 -> 22, of which waited for: 1 -> 6; matrix products, arithmetic and copies ran while one was open for 2% -> 28% of each run, Pallas kernels for 0% -> 0%
where the time goes in v1:
time: 88.5 us; the launch traced here: 88.2 us
  starting transfers between devices  44.7 us (51%)
  other arithmetic  17.4 us (20%)
  local copies, waits for them, and re-layouts  12.7 us (14%)
  waiting for transfers between devices  12.5 us (14%)
    ppermute x13, starting transfers between devices, swapped(): lax.ppermute(array, axis, [(i, i ^ mask) for i in range(lax.axis_size(axi...  25.2 us
    ppermute x6, starting transfers between devices, onward(): return lax.ppermute(array, (Y, CORE), pairs)  14.2 us
    dynamic_update_slice x10, local copies, waits for them, and re-layouts, put(): return lax.dynamic_update_slice(out, block, (at, jnp.int32(0)))  12.7 us
    dynamic_update_slice x6, other arithmetic, put(): return lax.dynamic_update_slice(out, block, (at, jnp.int32(0)))  10.5 us
    ppermute x3, waiting for transfers between devices, shifted(): return lax.ppermute(array, axis, [(i, (i + step) % n) for i in range(n)])  7.64 us
    ppermute x3, starting transfers between devices, shifted(): return lax.ppermute(array, axis, [(i, (i + step) % n) for i in range(n)])  5.24 us
    ppermute x13, waiting for transfers between devices, swapped(): lax.ppermute(array, axis, [(i, i ^ mask) for i in range(lax.axis_size(axi...  4.88 us
    reduce_sum x1, other arithmetic, body(): su = jnp.sum(jnp.abs(fresh_up), axis=0)  3.36 us
  transfers between devices with their start and end apart: 22, of which 6 were waited for; matrix products, arithmetic and copies ran while one was open for 28% of the time, Pallas kernels for 0%

profile of v1, /device:TPU:1, one launch (start us, length us, event | category | flops | bytes accessed | tf_op | source)
XLA Modules:
  0.0 88.2 jit_solution(1710723768754288047)
XLA Ops:
  1.5 3.4 %abs_reduce_fusion = (f32[768]{0:T(1024)S(1)}, f32[512,768]{1,0:T(8,128)S(1)}, f32[768]{0:T(1024)S(1)}, f32[512,768]{1,0:T(8,128)S(1)}) fusion(f32[512,768]{1,0:T(8,128)} %param.8, f32[512,768]{1,0:T(8,128)} %param.9, f32[512,768]{1,0:T(8,128)} %param.6, f32[512,768]{1,0:T(8,128)} %param.7), kind=kLoop, calls=%fused_computation.8 | loop fusion | flops 3930624 | bytes 9443328 | tf_op jit(solution)/shard_map/reduce_sum | solution.py:59
  4.9 1.5 %collective-permute-start.1 = (f32[5632]{0:T(1024)S(1)}, f32[5632]{0:T(1024)S(1)}, u32[]{:S(2)}, u32[]{:S(2)}) collective-permute-start(f32[5632]{0:T(1024)S(1)} %pad_maximum_fusion.1), channel_id=1, source_target_pairs={{0,16},{16,0},{1,17},{17,1},{2,18},{18,2},{3,19},{19,3},{4,20},{20... | collective-permute-start | bytes 67592 | tf_op jit(solution)/shard_map/ppermute | solution.py:22
  6.4 1.0 %multiply_convert_fusion.1 = f16[512,768]{1,0:T(8,128)(2,1)} fusion(f32[512,768]{1,0:T(8,128)S(1)} %get-tuple-element.26, f32[768]{0:T(1024)S(1)} %maximum_divide_fusion), kind=kLoop, calls=%fused_computation.1 | loop fusion | flops 786432 | bytes 2362368 | tf_op jit(solution)/shard_map/convert_element_type | solution.py:45
  7.5 2.8 %collective-permute-start.12 = (f16[512,768]{1,0:T(8,128)(2,1)}, f16[512,768]{1,0:T(8,128)(2,1)}, u32[]{:S(2)}, u32[]{:S(2)}) collective-permute-start(f16[512,768]{1,0:T(8,128)(2,1)} %multiply_convert_fusion.1), channel_id=1, source_target_pairs={{0,32},{16,112},{32,64},{48,16},{64,96},{80,48},{96,0},{112,80},{1... | collective-permute-start | bytes 2359304 | tf_op jit(solution)/shard_map/ppermute | solution.py:27
  11.2 1.9 %collective-permute-start.4 = (f32[7168]{0:T(1024)S(1)}, f32[7168]{0:T(1024)S(1)}, u32[]{:S(2)}, u32[]{:S(2)}) collective-permute-start(f32[7168]{0:T(1024)S(1)} %pad_maximum_fusion), channel_id=1, source_target_pairs={{0,96},{32,0},{64,32},{96,64},{1,97},{33,1},{65,33},{97,65},{2,98}... | collective-permute-start | bytes 86024 | tf_op jit(solution)/shard_map/ppermute | solution.py:18
  13.1 1.0 %multiply_convert_fusion.3 = f16[512,768]{1,0:T(8,128)(2,1)} fusion(f32[512,768]{1,0:T(8,128)S(1)} %get-tuple-element.30, f32[768]{0:T(1024)S(1)} %maximum_divide_fusion.1), kind=kLoop, calls=%fused_computation.5 | loop fusion | flops 786432 | bytes 2362368 | tf_op jit(solution)/shard_map/convert_element_type | solution.py:45
  14.1 0.9 %collective-permute-done.3 = f32[7168]{0:T(1024)S(1)} collective-permute-done((f32[7168]{0:T(1024)S(1)}, f32[7168]{0:T(1024)S(1)}, u32[]{:S(2)}, u32[]{:S(2)}) %collective-permute-start.3) | collective-permute-done | bytes 28704 | tf_op jit(solution)/shard_map/ppermute | solution.py:18
  15.1 5.0 %collective-permute-done.4 = f32[7168]{0:T(1024)S(1)} collective-permute-done((f32[7168]{0:T(1024)S(1)}, f32[7168]{0:T(1024)S(1)}, u32[]{:S(2)}, u32[]{:S(2)}) %collective-permute-start.4) | collective-permute-done | bytes 28704 | tf_op jit(solution)/shard_map/ppermute | solution.py:18
  20.1 2.5 %collective-permute-start.2 = (f32[5632]{0:T(1024)S(1)}, f32[5632]{0:T(1024)S(1)}, u32[]{:S(2)}, u32[]{:S(2)}) collective-permute-start(f32[5632]{0:T(1024)S(1)} %fusion.7), channel_id=1, source_target_pairs={{0,64},{32,96},{64,0},{96,32},{1,65},{33,97},{65,1},{97,33},{2,66}... | collective-permute-start | bytes 67592 | tf_op jit(solution)/shard_map/ppermute | solution.py:18
  22.6 1.7 %collective-permute-done.2 = f32[5632]{0:T(1024)S(1)} collective-permute-done((f32[5632]{0:T(1024)S(1)}, f32[5632]{0:T(1024)S(1)}, u32[]{:S(2)}, u32[]{:S(2)}) %collective-permute-start.2) | collective-permute-done | bytes 22560 | tf_op jit(solution)/shard_map/ppermute | solution.py:18
  24.3 2.4 %constant_dynamic-update-slice_fusion.6 = (bf16[4096,768]{1,0:T(8,128)(2,1)}, bf16[512,768]{1,0:T(8,128)(2,1)S(1)}) fusion(bf16[4096,768]{1,0:T(8,128)(2,1)} %get-tuple-element.10, s32[]{:T(128)S(6)} %select_n.48, f32[512,768]{1,0:T(8,128)} %collective-permute-done.11, f32[768]{0:T(1024)S(1)} %get-tuple-element.14), kind=kLoop, calls=%fused_computation.36 | loop fusion | flops 786432 | bytes 3148804 | tf_op jit(solution)/shard_map/dynamic_update_slice | solution.py:85
  26.7 6.3 %collective-permute-start.14 = (bf16[512,768]{1,0:T(8,128)(2,1)S(1)}, bf16[512,768]{1,0:T(8,128)(2,1)}, u32[]{:S(2)}, u32[]{:S(2)}) collective-permute-start(bf16[512,768]{1,0:T(8,128)(2,1)S(1)} %get-tuple-element.16), channel_id=1, source_target_pairs={{0,32},{16,112},{32,64},{48,16},{64,96},{80,48},{96,0},{112,80},{1... | collective-permute-start | bytes 2359304 | tf_op jit(solution)/shard_map/ppermute | solution.py:27
  33.1 2.4 %constant_dynamic-update-slice_fusion.13 = (bf16[4096,768]{1,0:T(8,128)(2,1)}, bf16[512,768]{1,0:T(8,128)(2,1)S(1)}) fusion(bf16[4096,768]{1,0:T(8,128)(2,1)} %get-tuple-element.9, s32[]{:T(128)S(6)} %select_n.48, f32[512,768]{1,0:T(8,128)} %collective-permute-done, f32[768]{0:T(1024)S(1)} %get-tuple-element.28), kind=kLoop, calls=%fused_computation.43 | loop fusion | flops 786432 | bytes 3148804 | tf_op jit(solution)/shard_map/dynamic_update_slice | solution.py:85
  35.5 1.0 %fusion.1 = bf16[4096,768]{1,0:T(8,128)(2,1)} fusion(bf16[4096,768]{1,0:T(8,128)(2,1)} %get-tuple-element.15, s32[]{:T(128)S(6)} %select_n.49, f32[512,768]{1,0:T(8,128)S(1)} %get-tuple-element.26, f32[768]{0:T(1024)S(1)} %get-tuple-element.14), kind=kLoop, calls=%fused_computation.13 | loop fusion | flops 786432 | bytes 2362372 | tf_op jit(solution)/shard_map/dynamic_update_slice | solution.py:85
  36.5 2.4 %constant_dynamic-update-slice_fusion.5 = (bf16[4096,768]{1,0:T(8,128)(2,1)}, bf16[512,768]{1,0:T(8,128)(2,1)}) fusion(bf16[4096,768]{1,0:T(8,128)(2,1)} %fusion.1, s32[]{:T(128)S(6)} %select_n.53, f32[768]{0:T(1024)S(1)} %get-tuple-element.13, f16[512,768]{1,0:T(8,128)(2,1)} %collective-permute-done.12), kind=kLoop, calls=%fused_computation.35 | loop fusion | flops 1179648 | bytes 2362372 | tf_op jit(solution)/shard_map/dynamic_update_slice | solution.py:85
  38.9 6.1 %collective-permute-start.13 = (bf16[512,768]{1,0:T(8,128)(2,1)}, bf16[512,768]{1,0:T(8,128)(2,1)S(1)}, u32[]{:S(2)}, u32[]{:S(2)}) collective-permute-start(bf16[512,768]{1,0:T(8,128)(2,1)} %get-tuple-element.12), channel_id=1, source_target_pairs={{0,16},{16,0},{1,17},{17,1},{2,18},{18,2},{3,19},{19,3},{4,20},{20... | collective-permute-start | bytes 2359304 | tf_op jit(solution)/shard_map/ppermute | solution.py:22
  45.0 1.0 %fusion = bf16[4096,768]{1,0:T(8,128)(2,1)} fusion(bf16[4096,768]{1,0:T(8,128)(2,1)} %get-tuple-element.21, s32[]{:T(128)S(6)} %select_n.49, f32[512,768]{1,0:T(8,128)S(1)} %get-tuple-element.30, f32[768]{0:T(1024)S(1)} %get-tuple-element.28), kind=kLoop, calls=%fused_computation.12 | loop fusion | flops 786432 | bytes 2362372 | tf_op jit(solution)/shard_map/dynamic_update_slice | solution.py:85
  46.0 1.3 %constant_dynamic-update-slice_fusion.12 = (bf16[4096,768]{1,0:T(8,128)(2,1)}, bf16[512,768]{1,0:T(8,128)(2,1)}) fusion(bf16[4096,768]{1,0:T(8,128)(2,1)} %fusion, s32[]{:T(128)S(6)} %select_n.53, f32[768]{0:T(1024)S(1)} %get-tuple-element.27, f16[512,768]{1,0:T(8,128)(2,1)S(1)} %collective-permute-done.5), kind=kLoop, calls=%fused_computation.42 | loop fusion | flops 1179648 | bytes 2362372 | tf_op jit(solution)/shard_map/dynamic_update_slice | solution.py:85
  47.3 2.1 %collective-permute-start.16 = (bf16[512,768]{1,0:T(8,128)(2,1)}, bf16[512,768]{1,0:T(8,128)(2,1)S(1)}, u32[]{:S(2)}, u32[]{:S(2)}) collective-permute-start(bf16[512,768]{1,0:T(8,128)(2,1)} %collective-permute-done.14), channel_id=1, source_target_pairs={{0,32},{16,112},{32,64},{48,16},{64,96},{80,48},{96,0},{112,80},{1... | collective-permute-start | bytes 2359304 | tf_op jit(solution)/shard_map/ppermute | solution.py:27
  49.4 2.2 %collective-permute-start.6 = (bf16[512,768]{1,0:T(8,128)(2,1)}, bf16[512,768]{1,0:T(8,128)(2,1)S(1)}, u32[]{:S(2)}, u32[]{:S(2)}) collective-permute-start(bf16[512,768]{1,0:T(8,128)(2,1)} %get-tuple-element.18), channel_id=1, source_target_pairs={{0,16},{16,0},{1,17},{17,1},{2,18},{18,2},{3,19},{19,3},{4,20},{20... | collective-permute-start | bytes 2359304 | tf_op jit(solution)/shard_map/ppermute | solution.py:22
  51.6 1.2 %collective-permute-start.18 = (bf16[4096]{0:T(1024)(128)(2,1)S(1)}, bf16[4096]{0:T(1024)(128)(2,1)S(1)}, u32[]{:S(2)}, u32[]{:S(2)}) collective-permute-start(bf16[4096]{0:T(1024)(128)(2,1)S(1)} %slice.65), channel_id=1, source_target_pairs={{0,1},{1,0},{2,3},{3,2},{4,5},{5,4},{6,7},{7,6},{8,9},{9,8},{10,11... | collective-permute-start | bytes 24584 | tf_op jit(solution)/shard_map/ppermute | solution.py:22
  52.8 3.0 %collective-permute-start.9 = (bf16[512,768]{1,0:T(8,128)(2,1)}, bf16[512,768]{1,0:T(8,128)(2,1)S(1)}, u32[]{:S(2)}, u32[]{:S(2)}) collective-permute-start(bf16[512,768]{1,0:T(8,128)(2,1)} %collective-permute-done.7), channel_id=1, source_target_pairs={{0,32},{16,112},{32,64},{48,16},{64,96},{80,48},{96,0},{112,80},{1... | collective-permute-start | bytes 2359304 | tf_op jit(solution)/shard_map/ppermute | solution.py:27
  55.8 1.9 %collective-permute-start.19 = (bf16[4096]{0:T(1024)(128)(2,1)S(1)}, bf16[4096]{0:T(1024)(128)(2,1)S(1)}, u32[]{:S(2)}, u32[]{:S(2)}) collective-permute-start(bf16[4096]{0:T(1024)(128)(2,1)S(1)} %slice_add_fusion.1), channel_id=1, source_target_pairs={{0,3},{1,2},{2,1},{3,0},{4,7},{5,6},{6,5},{7,4},{8,11},{9,10},{10,... | collective-permute-start | bytes 24584 | tf_op jit(solution)/shard_map/ppermute | solution.py:22
  57.7 2.2 %collective-permute-done.19 = bf16[4096]{0:T(1024)(128)(2,1)S(1)} collective-permute-done((bf16[4096]{0:T(1024)(128)(2,1)S(1)}, bf16[4096]{0:T(1024)(128)(2,1)S(1)}, u32[]{:S(2)}, u32[]{:S(2)}) %collective-permute-start.19) | collective-permute-done | bytes 8224 | tf_op jit(solution)/shard_map/ppermute | solution.py:22
  59.9 1.6 %collective-permute-start.20 = (bf16[4096]{0:T(1024)(128)(2,1)S(1)}, bf16[4096]{0:T(1024)(128)(2,1)S(1)}, u32[]{:S(2)}, u32[]{:S(2)}) collective-permute-start(bf16[4096]{0:T(1024)(128)(2,1)S(1)} %add.158), channel_id=1, source_target_pairs={{0,4},{4,0},{8,12},{12,8},{1,5},{5,1},{9,13},{13,9},{2,6},{6,2},{1... | collective-permute-start | bytes 24584 | tf_op jit(solution)/shard_map/ppermute | solution.py:22
  61.5 1.3 %collective-permute-done.20 = bf16[4096]{0:T(1024)(128)(2,1)S(1)} collective-permute-done((bf16[4096]{0:T(1024)(128)(2,1)S(1)}, bf16[4096]{0:T(1024)(128)(2,1)S(1)}, u32[]{:S(2)}, u32[]{:S(2)}) %collective-permute-start.20) | collective-permute-done | bytes 8224 | tf_op jit(solution)/shard_map/ppermute | solution.py:22
  62.9 3.6 %collective-permute-start.21 = (bf16[4096]{0:T(1024)(128)(2,1)S(1)}, bf16[4096]{0:T(1024)(128)(2,1)S(1)}, u32[]{:S(2)}, u32[]{:S(2)}) collective-permute-start(bf16[4096]{0:T(1024)(128)(2,1)S(1)} %add.159), channel_id=1, source_target_pairs={{0,12},{4,8},{8,4},{12,0},{1,13},{5,9},{9,5},{13,1},{2,14},{6,10},... | collective-permute-start | bytes 24584 | tf_op jit(solution)/shard_map/ppermute | solution.py:22
  66.4 1.3 %collective-permute-done.21 = bf16[4096]{0:T(1024)(128)(2,1)S(1)} collective-permute-done((bf16[4096]{0:T(1024)(128)(2,1)S(1)}, bf16[4096]{0:T(1024)(128)(2,1)S(1)}, u32[]{:S(2)}, u32[]{:S(2)}) %collective-permute-start.21) | collective-permute-done | bytes 8224 | tf_op jit(solution)/shard_map/ppermute | solution.py:22
  67.8 6.5 %collective-permute-start.15 = (bf16[512,768]{1,0:T(8,128)(2,1)}, bf16[512,768]{1,0:T(8,128)(2,1)}, u32[]{:S(2)}, u32[]{:S(2)}) collective-permute-start(bf16[512,768]{1,0:T(8,128)(2,1)} %collective-permute-done.14), channel_id=1, source_target_pairs={{0,16},{16,0},{1,17},{17,1},{2,18},{18,2},{3,19},{19,3},{4,20},{20... | collective-permute-start | bytes 2359304 | tf_op jit(solution)/shard_map/ppermute | solution.py:22
  75.9 2.1 %constant_dynamic-update-slice_fusion.3 = bf16[4096,768]{1,0:T(8,128)(2,1)} fusion(bf16[4096,768]{1,0:T(8,128)(2,1)} %constant_dynamic-update-slice_fusion.4, bf16[512,768]{1,0:T(8,128)(2,1)} %collective-permute-done.14, s32[]{:T(128)S(6)} %select_n.55), kind=kLoop, calls=%fused_computation.33 | loop fusion | bytes 1572868 | tf_op jit(solution)/shard_map/dynamic_update_slice | solution.py:85
  79.4 2.1 %constant_dynamic-update-slice_fusion.10 = bf16[4096,768]{1,0:T(8,128)(2,1)} fusion(bf16[4096,768]{1,0:T(8,128)(2,1)} %constant_dynamic-update-slice_fusion.11, bf16[512,768]{1,0:T(8,128)(2,1)} %collective-permute-done.7, s32[]{:T(128)S(6)} %select_n.55), kind=kLoop, calls=%fused_computation.40 | loop fusion | bytes 1572868 | tf_op jit(solution)/shard_map/dynamic_update_slice | solution.py:85
  81.4 2.1 %constant_dynamic-update-slice_fusion.2 = bf16[4096,768]{1,0:T(8,128)(2,1)} fusion(bf16[4096,768]{1,0:T(8,128)(2,1)} %constant_dynamic-update-slice_fusion.3, bf16[512,768]{1,0:T(8,128)(2,1)} %collective-permute-done.15, s32[]{:T(128)S(6)} %select_n.56), kind=kLoop, calls=%fused_computation.32 | loop fusion | bytes 1572868 | tf_op jit(solution)/shard_map/dynamic_update_slice | solution.py:85
  (55 shorter events, 9.6 us)
Async XLA Ops:
  4.8 31.7 %copy-start = (f32[512,768]{1,0:T(8,128)}, f32[512,768]{1,0:T(8,128)S(1)}, u32[]{:S(2)}) copy-start(f32[512,768]{1,0:T(8,128)S(1)} %get-tuple-element.26) | copy-start | bytes 4718596
  4.8 40.2 %copy-start.1 = (f32[512,768]{1,0:T(8,128)}, f32[512,768]{1,0:T(8,128)S(1)}, u32[]{:S(2)}) copy-start(f32[512,768]{1,0:T(8,128)S(1)} %get-tuple-element.30) | copy-start | bytes 4718596
  4.9 5.5 %collective-permute-start.1 = (f32[5632]{0:T(1024)S(1)}, f32[5632]{0:T(1024)S(1)}, u32[]{:S(2)}, u32[]{:S(2)}) collective-permute-start(f32[5632]{0:T(1024)S(1)} %pad_maximum_fusion.1), channel_id=1, source_target_pairs={{0,16},{16,0},{1,17},{17,1},{2,18},{18,2},{3,19},{19,3},{4,20},{20... | collective-permute-start | bytes 67592 | tf_op jit(solution)/shard_map/ppermute | solution.py:22
  6.3 18.0 %collective-permute-start.11 = (f32[512,768]{1,0:T(8,128)S(1)}, f32[512,768]{1,0:T(8,128)}, u32[]{:S(2)}, u32[]{:S(2)}) collective-permute-start(f32[512,768]{1,0:T(8,128)S(1)} %get-tuple-element.26), channel_id=1, source_target_pairs={{0,16},{16,0},{1,17},{17,1},{2,18},{18,2},{3,19},{19,3},{4,20},{20... | collective-permute-start | bytes 4718600 | tf_op jit(solution)/shard_map/ppermute | solution.py:22
  7.5 29.0 %collective-permute-start.12 = (f16[512,768]{1,0:T(8,128)(2,1)}, f16[512,768]{1,0:T(8,128)(2,1)}, u32[]{:S(2)}, u32[]{:S(2)}) collective-permute-start(f16[512,768]{1,0:T(8,128)(2,1)} %multiply_convert_fusion.1), channel_id=1, source_target_pairs={{0,32},{16,112},{32,64},{48,16},{64,96},{80,48},{96,0},{112,80},{1... | collective-permute-start | bytes 2359304 | tf_op jit(solution)/shard_map/ppermute | solution.py:27
  10.3 22.8 %collective-permute-start = (f32[512,768]{1,0:T(8,128)S(1)}, f32[512,768]{1,0:T(8,128)}, u32[]{:S(2)}, u32[]{:S(2)}) collective-permute-start(f32[512,768]{1,0:T(8,128)S(1)} %get-tuple-element.30), channel_id=1, source_target_pairs={{0,16},{16,0},{1,17},{17,1},{2,18},{18,2},{3,19},{19,3},{4,20},{20... | collective-permute-start | bytes 4718600 | tf_op jit(solution)/shard_map/ppermute | solution.py:22
  10.3 4.7 %collective-permute-start.3 = (f32[7168]{0:T(1024)S(1)}, f32[7168]{0:T(1024)S(1)}, u32[]{:S(2)}, u32[]{:S(2)}) collective-permute-start(f32[7168]{0:T(1024)S(1)} %pad_maximum_fusion), channel_id=1, source_target_pairs={{0,32},{32,64},{64,96},{96,0},{1,33},{33,65},{65,97},{97,1},{2,34}... | collective-permute-start | bytes 86024 | tf_op jit(solution)/shard_map/ppermute | solution.py:18
  11.2 8.8 %collective-permute-start.4 = (f32[7168]{0:T(1024)S(1)}, f32[7168]{0:T(1024)S(1)}, u32[]{:S(2)}, u32[]{:S(2)}) collective-permute-start(f32[7168]{0:T(1024)S(1)} %pad_maximum_fusion), channel_id=1, source_target_pairs={{0,96},{32,0},{64,32},{96,64},{1,97},{33,1},{65,33},{97,65},{2,98}... | collective-permute-start | bytes 86024 | tf_op jit(solution)/shard_map/ppermute | solution.py:18
  15.1 30.9 %collective-permute-start.5 = (f16[512,768]{1,0:T(8,128)(2,1)}, f16[512,768]{1,0:T(8,128)(2,1)S(1)}, u32[]{:S(2)}, u32[]{:S(2)}) collective-permute-start(f16[512,768]{1,0:T(8,128)(2,1)} %multiply_convert_fusion.3), channel_id=1, source_target_pairs={{0,32},{16,112},{32,64},{48,16},{64,96},{80,48},{96,0},{112,80},{1... | collective-permute-start | bytes 2359304 | tf_op jit(solution)/shard_map/ppermute | solution.py:27
  20.1 4.2 %collective-permute-start.2 = (f32[5632]{0:T(1024)S(1)}, f32[5632]{0:T(1024)S(1)}, u32[]{:S(2)}, u32[]{:S(2)}) collective-permute-start(f32[5632]{0:T(1024)S(1)} %fusion.7), channel_id=1, source_target_pairs={{0,64},{32,96},{64,0},{96,32},{1,65},{33,97},{65,1},{97,33},{2,66}... | collective-permute-start | bytes 67592 | tf_op jit(solution)/shard_map/ppermute | solution.py:18
  24.3 21.7 %copy-start.2 = (f32[768]{0:T(1024)}, f32[768]{0:T(1024)S(1)}, u32[]{:S(2)}) copy-start(f32[768]{0:T(1024)S(1)} %get-tuple-element.14) | copy-start | bytes 9220
  24.3 21.7 %copy-start.3 = (f32[768]{0:T(1024)}, f32[768]{0:T(1024)S(1)}, u32[]{:S(2)}) copy-start(f32[768]{0:T(1024)S(1)} %get-tuple-element.28) | copy-start | bytes 9220
  26.7 20.6 %collective-permute-start.14 = (bf16[512,768]{1,0:T(8,128)(2,1)S(1)}, bf16[512,768]{1,0:T(8,128)(2,1)}, u32[]{:S(2)}, u32[]{:S(2)}) collective-permute-start(bf16[512,768]{1,0:T(8,128)(2,1)S(1)} %get-tuple-element.16), channel_id=1, source_target_pairs={{0,32},{16,112},{32,64},{48,16},{64,96},{80,48},{96,0},{112,80},{1... | collective-permute-start | bytes 2359304 | tf_op jit(solution)/shard_map/ppermute | solution.py:27
  35.5 17.3 %collective-permute-start.7 = (bf16[512,768]{1,0:T(8,128)(2,1)S(1)}, bf16[512,768]{1,0:T(8,128)(2,1)}, u32[]{:S(2)}, u32[]{:S(2)}) collective-permute-start(bf16[512,768]{1,0:T(8,128)(2,1)S(1)} %get-tuple-element.22), channel_id=1, source_target_pairs={{0,32},{16,112},{32,64},{48,16},{64,96},{80,48},{96,0},{112,80},{1... | collective-permute-start | bytes 2359304 | tf_op jit(solution)/shard_map/ppermute | solution.py:27
  38.9 36.0 %collective-permute-start.13 = (bf16[512,768]{1,0:T(8,128)(2,1)}, bf16[512,768]{1,0:T(8,128)(2,1)S(1)}, u32[]{:S(2)}, u32[]{:S(2)}) collective-permute-start(bf16[512,768]{1,0:T(8,128)(2,1)} %get-tuple-element.12), channel_id=1, source_target_pairs={{0,16},{16,0},{1,17},{17,1},{2,18},{18,2},{3,19},{19,3},{4,20},{20... | collective-permute-start | bytes 2359304 | tf_op jit(solution)/shard_map/ppermute | solution.py:22
  47.3 30.6 %collective-permute-start.16 = (bf16[512,768]{1,0:T(8,128)(2,1)}, bf16[512,768]{1,0:T(8,128)(2,1)S(1)}, u32[]{:S(2)}, u32[]{:S(2)}) collective-permute-start(bf16[512,768]{1,0:T(8,128)(2,1)} %collective-permute-done.14), channel_id=1, source_target_pairs={{0,32},{16,112},{32,64},{48,16},{64,96},{80,48},{96,0},{112,80},{1... | collective-permute-start | bytes 2359304 | tf_op jit(solution)/shard_map/ppermute | solution.py:27
  49.4 29.0 %collective-permute-start.6 = (bf16[512,768]{1,0:T(8,128)(2,1)}, bf16[512,768]{1,0:T(8,128)(2,1)S(1)}, u32[]{:S(2)}, u32[]{:S(2)}) collective-permute-start(bf16[512,768]{1,0:T(8,128)(2,1)} %get-tuple-element.18), channel_id=1, source_target_pairs={{0,16},{16,0},{1,17},{17,1},{2,18},{18,2},{3,19},{19,3},{4,20},{20... | collective-permute-start | bytes 2359304 | tf_op jit(solution)/shard_map/ppermute | solution.py:22
  51.6 4.2 %collective-permute-start.18 = (bf16[4096]{0:T(1024)(128)(2,1)S(1)}, bf16[4096]{0:T(1024)(128)(2,1)S(1)}, u32[]{:S(2)}, u32[]{:S(2)}) collective-permute-start(bf16[4096]{0:T(1024)(128)(2,1)S(1)} %slice.65), channel_id=1, source_target_pairs={{0,1},{1,0},{2,3},{3,2},{4,5},{5,4},{6,7},{7,6},{8,9},{9,8},{10,11... | collective-permute-start | bytes 24584 | tf_op jit(solution)/shard_map/ppermute | solution.py:22
  52.8 26.5 %collective-permute-start.9 = (bf16[512,768]{1,0:T(8,128)(2,1)}, bf16[512,768]{1,0:T(8,128)(2,1)S(1)}, u32[]{:S(2)}, u32[]{:S(2)}) collective-permute-start(bf16[512,768]{1,0:T(8,128)(2,1)} %collective-permute-done.7), channel_id=1, source_target_pairs={{0,32},{16,112},{32,64},{48,16},{64,96},{80,48},{96,0},{112,80},{1... | collective-permute-start | bytes 2359304 | tf_op jit(solution)/shard_map/ppermute | solution.py:27
  55.8 4.1 %collective-permute-start.19 = (bf16[4096]{0:T(1024)(128)(2,1)S(1)}, bf16[4096]{0:T(1024)(128)(2,1)S(1)}, u32[]{:S(2)}, u32[]{:S(2)}) collective-permute-start(bf16[4096]{0:T(1024)(128)(2,1)S(1)} %slice_add_fusion.1), channel_id=1, source_target_pairs={{0,3},{1,2},{2,1},{3,0},{4,7},{5,6},{6,5},{7,4},{8,11},{9,10},{10,... | collective-permute-start | bytes 24584 | tf_op jit(solution)/shard_map/ppermute | solution.py:22
  59.9 3.0 %collective-permute-start.20 = (bf16[4096]{0:T(1024)(128)(2,1)S(1)}, bf16[4096]{0:T(1024)(128)(2,1)S(1)}, u32[]{:S(2)}, u32[]{:S(2)}) collective-permute-start(bf16[4096]{0:T(1024)(128)(2,1)S(1)} %add.158), channel_id=1, source_target_pairs={{0,4},{4,0},{8,12},{12,8},{1,5},{5,1},{9,13},{13,9},{2,6},{6,2},{1... | collective-permute-start | bytes 24584 | tf_op jit(solution)/shard_map/ppermute | solution.py:22
  62.9 4.9 %collective-permute-start.21 = (bf16[4096]{0:T(1024)(128)(2,1)S(1)}, bf16[4096]{0:T(1024)(128)(2,1)S(1)}, u32[]{:S(2)}, u32[]{:S(2)}) collective-permute-start(bf16[4096]{0:T(1024)(128)(2,1)S(1)} %add.159), channel_id=1, source_target_pairs={{0,12},{4,8},{8,4},{12,0},{1,13},{5,9},{9,5},{13,1},{2,14},{6,10},... | collective-permute-start | bytes 24584 | tf_op jit(solution)/shard_map/ppermute | solution.py:22
  67.8 13.7 %collective-permute-start.15 = (bf16[512,768]{1,0:T(8,128)(2,1)}, bf16[512,768]{1,0:T(8,128)(2,1)}, u32[]{:S(2)}, u32[]{:S(2)}) collective-permute-start(bf16[512,768]{1,0:T(8,128)(2,1)} %collective-permute-done.14), channel_id=1, source_target_pairs={{0,16},{16,0},{1,17},{17,1},{2,18},{18,2},{3,19},{19,3},{4,20},{20... | collective-permute-start | bytes 2359304 | tf_op jit(solution)/shard_map/ppermute | solution.py:22
  74.9 9.5 %collective-permute-start.8 = (bf16[512,768]{1,0:T(8,128)(2,1)}, bf16[512,768]{1,0:T(8,128)(2,1)S(1)}, u32[]{:S(2)}, u32[]{:S(2)}) collective-permute-start(bf16[512,768]{1,0:T(8,128)(2,1)} %collective-permute-done.7), channel_id=1, source_target_pairs={{0,16},{16,0},{1,17},{17,1},{2,18},{18,2},{3,19},{19,3},{4,20},{20... | collective-permute-start | bytes 2359304 | tf_op jit(solution)/shard_map/ppermute | solution.py:22
  77.9 8.4 %collective-permute-start.17 = (bf16[512,768]{1,0:T(8,128)(2,1)S(1)}, bf16[512,768]{1,0:T(8,128)(2,1)S(1)}, u32[]{:S(2)}, u32[]{:S(2)}) collective-permute-start(bf16[512,768]{1,0:T(8,128)(2,1)S(1)} %collective-permute-done.16), channel_id=1, source_target_pairs={{0,16},{16,0},{1,17},{17,1},{2,18},{18,2},{3,19},{19,3},{4,20},{20... | collective-permute-start | bytes 2359304 | tf_op jit(solution)/shard_map/ppermute | solution.py:22
  79.4 7.9 %collective-permute-start.10 = (bf16[512,768]{1,0:T(8,128)(2,1)S(1)}, bf16[512,768]{1,0:T(8,128)(2,1)S(1)}, u32[]{:S(2)}, u32[]{:S(2)}) collective-permute-start(bf16[512,768]{1,0:T(8,128)(2,1)S(1)} %collective-permute-done.9), channel_id=1, source_target_pairs={{0,16},{16,0},{1,17},{17,1},{2,18},{18,2},{3,19},{19,3},{4,20},{20... | collective-permute-start | bytes 2359304 | tf_op jit(solution)/shard_map/ppermute | solution.py:22
